TPU v7x, 32 devices: a whole 2x2x4 slice. The times are simulated.
32 devices in a mesh: win: 32 (over z, y, x, core).
Axes of the slice: x: 2, y: 2, z: 4, core: 2. Of those that a mesh axis runs over, the one named last changes fastest.
Arguments:
- point_rows: int32 [64, 32768], P('win'), may hold values from 0 to 31
- point_cols: int32 [64, 32768], P('win'), may hold values from 0 to 1023
- point_chans: int32 [64, 32768], P('win'), may hold values from 0 to 3
- point_weights: bfloat16 [64, 32768], P('win'), may hold values from 0.25 to 4
- decay: float32 [64, 4], P('win'), may hold values from 0.3 to 1
Outputs:
- heat: float32 [64, 4, 32, 1024], P('win')
All inputs are finite; a program needn't handle non-finite values.
Results may differ from a plain program's by a relative error of at most 0.0003.
Values sent between devices are 32-bit elements; how exact they have to be, the bound alone decides.
A program may use at most 64 MiB of HBM per device.

v0:
```python
import functools

import jax
import jax.numpy as jnp
from jax import lax
from jax.experimental import pallas as pl
from jax.experimental.pallas import tpu as pltpu
from jax.sharding import PartitionSpec as P

IMAGE_LAYERS = 4
COLS = 1024
ROWS = 32


def one_hot(index, size, on, points):
    spread = jnp.broadcast_to(index.astype(jnp.float32), (16, points)).astype(jnp.bfloat16)
    slots = lax.broadcasted_iota(jnp.int32, (16, points), 0).astype(jnp.float32).astype(jnp.bfloat16)
    off = jnp.zeros((16, points), jnp.bfloat16)
    return jnp.concatenate(
        [jnp.where(spread == slots + jnp.bfloat16(16.0 * g), on, off) for g in range(size // 16)], axis=0
    )


def bin_kernel(points, rows_ref, cols_ref, chans_ref, weights_ref, hist_ref):
    windows, total = rows_ref.shape
    slots = IMAGE_LAYERS * ROWS
    for window in range(windows):
        hist_ref[window] = jnp.zeros((slots, COLS), jnp.float32)

        def step(i, carry):
            here = pl.ds(pl.multiple_of(i * points, points), points)
            take = lambda ref: ref[window : window + 1, here]
            cols = take(cols_ref)
            cell = take(chans_ref) * ROWS + take(rows_ref) + (cols // 256) * slots
            weights = jnp.broadcast_to(take(weights_ref).astype(jnp.float32), (16, points)).astype(jnp.bfloat16)
            right = one_hot(cols % 256, 256, weights, points)
            for first in range(0, slots * COLS // 256, 256):
                left = one_hot(cell - first, 256, jnp.ones((16, points), jnp.bfloat16), points)
                part = lax.dot_general(
                    left, right, (((1,), (1,)), ((), ())), preferred_element_type=jnp.float32
                )
                for j in range(256 // slots):
                    at = (first // slots + j) * 256
                    hist_ref[window, :, at : at + 256] += part[j * slots : (j + 1) * slots]
            return carry

        lax.fori_loop(0, total // points, step, 0)


def bin_points(point_rows, point_cols, point_chans, point_weights):
    windows, total = point_rows.shape
    hist = pl.pallas_call(
        functools.partial(bin_kernel, min(4096, total)),
        out_shape=jax.ShapeDtypeStruct((windows, IMAGE_LAYERS * ROWS, COLS), jnp.float32),
        in_specs=[pl.BlockSpec(memory_space=pltpu.VMEM)] * 4,
        out_specs=pl.BlockSpec(memory_space=pltpu.VMEM),
        compiler_params=pltpu.CompilerParams(vmem_limit_bytes=48 * 2**20),
    )(point_rows, point_cols, point_chans, point_weights)
    return hist.reshape(windows, IMAGE_LAYERS, ROWS, COLS)


def affine_cells(earlier, later):
    return (earlier[0] * later[0], later[0] * earlier[1] + later[1])


def spread_factors(factors, first_cell, piece):
    channel_of = (first_cell + jnp.arange(piece, dtype=jnp.int32)) // (ROWS * COLS)
    spread = jnp.zeros((factors.shape[0], piece), jnp.float32)
    for channel in range(IMAGE_LAYERS):
        spread = spread + jnp.where(
            channel_of[None, :] == channel, factors[:, channel][:, None], 0.0
        )
    return spread


def finish(running, decay, hist):
    outputs = []
    for window in range(hist.shape[0]):
        running = decay[window][:, None, None] * running + hist[window]
        outputs.append(running)
    return jnp.stack(outputs, 0)


def summarize(decay, hist):
    shard_multiplier = jnp.ones((IMAGE_LAYERS,), jnp.float32)
    local_canvas = jnp.zeros((IMAGE_LAYERS, ROWS, COLS), jnp.float32)
    for window in range(hist.shape[0]):
        local_canvas = decay[window][:, None, None] * local_canvas + hist[window]
        shard_multiplier = shard_multiplier * decay[window]
    return (shard_multiplier, local_canvas)


def local(point_rows, point_cols, point_chans, point_weights, decay):
    cells = IMAGE_LAYERS * ROWS * COLS
    hist = bin_points(point_rows, point_cols, point_chans, point_weights)
    shard_multiplier, local_canvas = summarize(decay, hist)
    all_factors = lax.all_gather(shard_multiplier[None, :], "win", axis=0, tiled=True)
    owned = lax.all_to_all(
        local_canvas.reshape(1, cells), "win", split_axis=1, concat_axis=0, tiled=True
    )
    piece = owned.shape[1]
    cell_decay = spread_factors(all_factors, lax.axis_index("win") * piece, piece)
    inclusive = lax.associative_scan(affine_cells, (cell_decay, owned), axis=0)
    exclusive = jnp.concatenate([jnp.zeros((1, piece), jnp.float32), inclusive[1][:-1]], 0)
    returned = lax.all_to_all(exclusive, "win", split_axis=0, concat_axis=1, tiled=True)
    return finish(returned.reshape(IMAGE_LAYERS, ROWS, COLS), decay, hist)


def solution(mesh):
    placed = (P("win", None), P("win", None), P("win", None), P("win", None), P("win", None))
    return jax.shard_map(
        local, mesh=mesh, in_specs=placed, out_specs=P("win", None, None, None), check_vma=False
    )
```

profile of v0, /device:TPU:0, one launch (start us, length us, event | category | flops | bytes accessed | tf_op | source)
XLA Modules:
  0.0 107.3 jit_solution(15030325366551125559)
XLA Ops:
  0.0 0.8 slice_bitcast_fusion.6
  0.8 0.9 copy-done
  1.8 0.9 copy-done.1
  2.7 0.9 copy-done.2
  3.7 0.9 copy-done.3
  4.6 20.8 %shard_map.55 = f32[2,128,1024]{2,1,0:T(8,128)S(1)} custom-call(s32[2,32768]{1,0:T(2,128)S(1)} %copy-done, s32[2,32768]{1,0:T(2,128)S(1)} %copy-done.1, s32[2,32768]{1,0:T(2,128)S(1)} %copy-done.2, bf16[2,32768]{1,0:T(2,128)(2,1)S(1)} %copy-done.3), custom_call_target="tpu_custom_call" | custom-call | tf_op jit(solution)/shard_map/pallas_call | solution.py:52
  25.4 0.1 fusion.9
  25.5 0.6 squeeze.19
  26.1 0.1 mul.116
  26.2 0.6 mul.117
  26.8 0.1 mul.119
  26.9 0.6 mul.120
  27.6 0.6 squeeze.18
  28.2 0.9 multiply_add_fusion.2
  29.1 7.3 %all-to-all-start = ((f32[1,32,4096]{2,0,1:T(1,128)}), f32[1,32,4096]{2,0,1:T(1,128)S(1)}, u32[]{:S(2)}, u32[]{:S(2)}) async-start(f32[1,32,4096]{2,0,1:T(1,128)} %bitcast.30), calls=%async_computation | async-start | bytes 1048576 | tf_op jit(solution)/shard_map/all_to_all | solution.py:98
  36.4 43.8 %all-gather = f32[32,1,4]{2,1,0:T(1,128)S(1)} all-gather(f32[1,1,4]{2,1,0:T(1,128)S(1)} %get-tuple-element.24), channel_id=1, replica_groups=mesh['win'=32] {'win'}, dimensions={0}, use_global_device_ids=true | all-gather | bytes 528 | tf_op jit(solution)/shard_map/all_gather | solution.py:97
  80.2 0.1 copy.9
  80.3 0.2 select_add_fusion
  80.5 0.2 slice.159
  80.7 0.1 slice.164
  80.9 0.1 slice.160
  81.0 0.3 copy.13
  81.3 0.2 slice.192
  81.5 0.1 slice.162
  81.7 0.8 slice.161
  82.5 1.0 fusion.10
  83.5 0.1 slice.170
  83.6 0.1 slice.166
  83.7 0.1 slice.168
  83.8 0.1 slice.167
  83.9 0.1 slice.171
  84.1 0.1 slice.176
  84.2 0.1 slice.172
  84.3 0.1 slice.188
  84.4 0.1 slice.174
  84.5 0.1 slice.173
  84.7 0.1 slice.180
  84.8 0.1 slice.179
  84.9 0.1 slice.178
  85.0 0.1 slice.182
  85.4 0.1 slice.190
  85.5 0.1 slice.165
  86.6 0.5 copy.10
  87.2 17.5 %all_to_all.26 = f32[32,1,4096]{2,1,0:T(1,128)S(1)} all-to-all(f32[32,1,4096]{2,1,0:T(1,128)S(1)} %copy.10), channel_id=1, replica_groups=mesh['win'=32] {'win'}, dimensions={0} | all-to-all | bytes 1048576 | tf_op jit(solution)/shard_map/all_to_all | solution.py:105
  104.7 1.2 %reduce = f32[32,4096]{1,0:T(8,128)S(1)} reduce(f32[32,1,4096]{2,1,0:T(1,128)S(1)} %all_to_all.26, f32[]{:T(128)} %constant.59), dimensions={1}, to_apply=%all_to_all.23.reduce_sub_computation | reduce | bytes 1048580 | tf_op jit(solution)/shard_map/all_to_all | solution.py:105
  105.9 0.1 reshape.143
  106.1 0.2 multiply_add_fusion
  106.3 1.0 pad_maximum_fusion
  (40 shorter events, 1.2 us)
Async XLA Ops:
  0.0 0.8 copy-start.4
  0.8 1.0 copy-start
  1.8 0.9 copy-start.1
  2.7 0.9 copy-start.2
  3.7 0.9 copy-start.3
  29.1 51.9 %all-to-all-start = ((f32[1,32,4096]{2,0,1:T(1,128)}), f32[1,32,4096]{2,0,1:T(1,128)S(1)}, u32[]{:S(2)}, u32[]{:S(2)}) async-start(f32[1,32,4096]{2,0,1:T(1,128)} %bitcast.30), calls=%async_computation | async-start | bytes 1048576 | tf_op jit(solution)/shard_map/all_to_all | solution.py:98
where the time goes:
time: 108 us; the launch traced here: 107 us
  blocking collectives  61.3 us (57%)
  Pallas kernels  20.8 us (19%)
  local copies, waits for them, and re-layouts  11.4 us (11%)
  starting transfers between devices  7.32 us (7%)
  other arithmetic  6.06 us (6%)
    all_gather x1, blocking collectives, local(): lax.all_gather(shard_multiplier[None, :], 'win', axis=0, tiled=True)  43.8 us
    pallas_call x1, Pallas kernels, bin_points(): pl.pallas_call(functools.partial(bin_kernel, min(4096, total)), out_shape...  20.8 us
    all_to_all x1, blocking collectives, local(): lax.all_to_all(exclusive, 'win', split_axis=0, concat_axis=1, tiled=True)  17.5 us
    all_to_all x1, starting transfers between devices, local(): lax.all_to_all(local_canvas.reshape(1, cells), 'win', split_axis=1, conca...  7.32 us
    unnamed x12, local copies, waits for them, and re-layouts  4.13 us
    slice x25, local copies, waits for them, and re-layouts, local(): inclusive = lax.associative_scan(affine_cells, (cell_decay, owned), axis=0)  3.29 us
  transfers between devices with their start and end apart: 1, of which 0 were waited for; matrix products, arithmetic and copies ran while one was open for 1% of the time, Pallas kernels for 0%

commit v1 on v0

v1 whole, which is shorter than its diff:
```python
import functools

import jax
import jax.numpy as jnp
from jax import lax
from jax.experimental import pallas as pl
from jax.experimental.pallas import tpu as pltpu
from jax.sharding import PartitionSpec as P

IMAGE_LAYERS = 4
COLS = 1024
ROWS = 32
SLOTS = IMAGE_LAYERS * ROWS
LANES = 128
SUBLANES = 8
PART = 256
CHUNK = 512
POINTS = 8192
MESH = pl.DeviceIdType.MESH


def one_hot(index, size, on, points):
    spread = jnp.broadcast_to(index.astype(jnp.float32), (16, points)).astype(jnp.bfloat16)
    slots = lax.broadcasted_iota(jnp.int32, (16, points), 0).astype(jnp.float32).astype(jnp.bfloat16)
    off = jnp.zeros((16, points), jnp.bfloat16)
    return jnp.concatenate(
        [jnp.where(spread == slots + jnp.bfloat16(16.0 * g), on, off) for g in range(size // 16)], axis=0
    )


def bin_step(rows_ref, cols_ref, chans_ref, weights_ref, hist, window, chunk, first, points):
    here = pl.ds(pl.multiple_of(first, points), points)
    take = lambda ref: ref[window : window + 1, here]
    cols = take(cols_ref)
    cell = take(chans_ref) * ROWS + take(rows_ref) + (cols // PART - chunk * (CHUNK // PART)) * SLOTS
    cell = jnp.clip(cell, -1, CHUNK // PART * SLOTS)
    weights = jnp.broadcast_to(take(weights_ref).astype(jnp.float32), (16, points)).astype(jnp.bfloat16)
    right = one_hot(cols % PART, PART, weights, points)
    left = one_hot(cell, CHUNK // PART * SLOTS, jnp.ones((16, points), jnp.bfloat16), points)
    part = lax.dot_general(left, right, (((1,), (1,)), ((), ())), preferred_element_type=jnp.float32)
    for j in range(CHUNK // PART):
        hist[window, chunk, :, j * PART : (j + 1) * PART] += part[j * SLOTS : (j + 1) * SLOTS]


def across(tile, width):
    return jnp.concatenate([tile] * (width // LANES), axis=1)


def kernel(
    n, size, points,
    rows_hbm, cols_hbm, chans_hbm, weights_hbm, decay_ref, out_hbm,
    rows_ref, cols_ref, chans_ref, weights_ref, hist, stage, inbox, total, earlier, carried, spread, back, prefix,
    load_sem, store_sem, go_send, go_recv, up_send, up_recv, back_send, back_recv,
):
    windows, count = rows_ref.shape
    groups = n // size
    piece = SLOTS // size
    chunks = COLS // CHUNK
    me = lax.axis_index("win")
    group, member = lax.div(me, size), lax.rem(me, size)
    mate = lambda k: group * size + lax.rem(member + k, size)

    loads = [
        pltpu.make_async_copy(source, target, load_sem.at[i])
        for i, (source, target) in enumerate(
            ((cols_hbm, cols_ref), (chans_hbm, chans_ref), (rows_hbm, rows_ref), (weights_hbm, weights_ref))
        )
    ]
    for load in loads:
        load.start()

    barrier = pltpu.get_barrier_semaphore()
    for k in range(1, size):
        pl.semaphore_signal(barrier, inc=1, device_id=(mate(k),), device_id_type=MESH)
    for k in range(1, groups):
        pl.semaphore_signal(barrier, inc=1, device_id=(lax.rem(me + k * size, n),), device_id_type=MESH)

    hist[...] = jnp.zeros(hist.shape, jnp.float32)
    for load in loads:
        load.wait()
    pl.semaphore_wait(barrier, size - 1 + groups - 1)

    def go(chunk, k):
        peer = lax.rem(member + k, size)
        return pltpu.make_async_remote_copy(
            src_ref=stage.at[chunk, peer], dst_ref=inbox.at[chunk, member],
            send_sem=go_send.at[chunk, k], recv_sem=go_recv.at[chunk, member],
            device_id=(mate(k),), device_id_type=MESH,
        )

    def come(chunk, k):
        peer = lax.rem(member + k, size)
        return pltpu.make_async_remote_copy(
            src_ref=stage.at[chunk, peer], dst_ref=inbox.at[chunk, peer],
            send_sem=go_send.at[chunk, k], recv_sem=go_recv.at[chunk, peer],
            device_id=(mate(k),), device_id_type=MESH,
        )

    def up(chunk, k, slot):
        return pltpu.make_async_remote_copy(
            src_ref=total.at[chunk], dst_ref=earlier.at[chunk, slot],
            send_sem=up_send.at[chunk, k], recv_sem=up_recv.at[chunk, slot],
            device_id=(lax.rem(me + k * size, n),), device_id_type=MESH,
        )

    def give(chunk, k):
        peer = lax.rem(member + k, size)
        return pltpu.make_async_remote_copy(
            src_ref=back.at[chunk, peer], dst_ref=prefix.at[chunk, member],
            send_sem=back_send.at[chunk, k], recv_sem=back_recv.at[chunk, member],
            device_id=(mate(k),), device_id_type=MESH,
        )

    def get(chunk, k):
        peer = lax.rem(member + k, size)
        return pltpu.make_async_remote_copy(
            src_ref=back.at[chunk, peer], dst_ref=prefix.at[chunk, peer],
            send_sem=back_send.at[chunk, k], recv_sem=back_recv.at[chunk, peer],
            device_id=(mate(k),), device_id_type=MESH,
        )

    def send_sums(chunk):
        for p in range(size):
            channel = p * piece // ROWS
            at = slice(p * piece, (p + 1) * piece)
            running = hist[0, chunk, at, :]
            factor = jnp.full((piece, LANES), decay_ref[0, channel], jnp.float32)
            for window in range(1, windows):
                running = decay_ref[window, channel] * running + hist[window, chunk, at, :]
                factor = factor * decay_ref[window, channel]
            stage[chunk, p, :, :CHUNK] = running
            stage[chunk, p, :, CHUNK:] = factor
        for k in range(1, size):
            go(chunk, k).start()
        inbox[chunk, member] = stage[chunk, member]

    def scan_group(chunk):
        for k in range(1, size):
            come(chunk, k).wait_recv()
        running = jnp.zeros((piece, CHUNK), jnp.float32)
        factor = jnp.ones((piece, LANES), jnp.float32)
        for m in range(size):
            back[chunk, m] = running
            spread[chunk, m] = factor
            by = inbox[chunk, m, :, CHUNK:]
            running = across(by, CHUNK) * running + inbox[chunk, m, :, :CHUNK]
            factor = factor * by
        total[chunk, :, :CHUNK] = running
        total[chunk, :, CHUNK:] = factor
        for k in range(1, groups):

            @pl.when(group + k < groups)
            def _():
                up(chunk, k, group).start()

    def send_back(chunk):
        if groups > 1:
            carried[...] = jnp.zeros((piece, CHUNK), jnp.float32)
            for g in range(groups - 1):

                @pl.when(g < group)
                def _():
                    up(chunk, 1, g).wait_recv()
                    by = earlier[chunk, g, :, CHUNK:]
                    carried[...] = across(by, CHUNK) * carried[...] + earlier[chunk, g, :, :CHUNK]

            @pl.when(group > 0)
            def _():
                before = carried[...]
                for m in range(size):
                    back[chunk, m] += across(spread[chunk, m], CHUNK) * before

        for k in range(1, size):
            give(chunk, k).start()
        prefix[chunk, member] = back[chunk, member]

    def store(chunk, window):
        return pltpu.make_async_copy(
            hist.at[window, chunk],
            out_hbm.at[window, :, pl.ds(chunk * CHUNK, CHUNK)],
            store_sem.at[chunk, window],
        )

    def finish(chunk):
        for k in range(1, size):
            get(chunk, k).wait_recv()
        for p in range(size):
            channel = p * piece // ROWS
            at = slice(p * piece, (p + 1) * piece)
            running = prefix[chunk, p]
            for window in range(windows):
                running = decay_ref[window, channel] * running + hist[window, chunk, at, :]
                hist[window, chunk, at, :] = running
        for window in range(windows):
            store(chunk, window).start()

    steps = count // points
    for chunk in range(chunks):
        for window in range(windows):

            def step(i, carry):
                if chunk > 0 and window == windows - 1:

                    @pl.when(i == steps // 4)
                    def _():
                        scan_group(chunk - 1)

                    @pl.when(i == steps - 1)
                    def _():
                        send_back(chunk - 1)

                bin_step(
                    rows_ref, cols_ref, chans_ref, weights_ref, hist, window, chunk, i * points, points
                )
                return carry

            lax.fori_loop(0, steps, step, 0)
        send_sums(chunk)
        if chunk > 0:
            finish(chunk - 1)
    scan_group(chunks - 1)
    send_back(chunks - 1)
    finish(chunks - 1)

    for chunk in range(chunks):
        for window in range(windows):
            store(chunk, window).wait()
        for k in range(1, size):
            go(chunk, k).wait_send()
            give(chunk, k).wait_send()
        for k in range(1, groups):

            @pl.when(group + k < groups)
            def _():
                up(chunk, k, group).wait_send()


def local(n, point_rows, point_cols, point_chans, point_weights, decay):
    windows, count = point_rows.shape
    size = max(s for s in range(1, SLOTS // SUBLANES + 1) if n % s == 0 and SLOTS % (s * SUBLANES) == 0)
    groups = n // size
    piece, chunks = SLOTS // size, COLS // CHUNK
    wide = CHUNK + LANES
    dma = pltpu.SemaphoreType.DMA
    heat = pl.pallas_call(
        functools.partial(kernel, n, size, min(POINTS, count)),
        out_shape=jax.ShapeDtypeStruct((windows, SLOTS, COLS), jnp.float32),
        in_specs=[pl.BlockSpec(memory_space=pl.ANY)] * 4 + [pl.BlockSpec(memory_space=pltpu.SMEM)],
        out_specs=pl.BlockSpec(memory_space=pl.ANY),
        scratch_shapes=[
            pltpu.VMEM((windows, count), jnp.int32),
            pltpu.VMEM((windows, count), jnp.int32),
            pltpu.VMEM((windows, count), jnp.int32),
            pltpu.VMEM((windows, count), jnp.bfloat16),
            pltpu.VMEM((windows, chunks, SLOTS, CHUNK), jnp.float32),
            pltpu.VMEM((chunks, size, piece, wide), jnp.float32),
            pltpu.VMEM((chunks, size, piece, wide), jnp.float32),
            pltpu.VMEM((chunks, piece, wide), jnp.float32),
            pltpu.VMEM((chunks, groups, piece, wide), jnp.float32),
            pltpu.VMEM((piece, CHUNK), jnp.float32),
            pltpu.VMEM((chunks, size, piece, LANES), jnp.float32),
            pltpu.VMEM((chunks, size, piece, CHUNK), jnp.float32),
            pltpu.VMEM((chunks, size, piece, CHUNK), jnp.float32),
            dma((4,)),
            dma((chunks, windows)),
            dma((chunks, size)),
            dma((chunks, size)),
            dma((chunks, groups)),
            dma((chunks, groups)),
            dma((chunks, size)),
            dma((chunks, size)),
        ],
        compiler_params=pltpu.CompilerParams(
            collective_id=0, has_side_effects=True, vmem_limit_bytes=56 * 2**20
        ),
    )(point_rows, point_cols, point_chans, point_weights, decay)
    return heat.reshape(windows, IMAGE_LAYERS, ROWS, COLS)


def solution(mesh):
    placed = (P("win", None), P("win", None), P("win", None), P("win", None), P("win", None))
    return jax.shard_map(
        functools.partial(local, mesh.shape["win"]),
        mesh=mesh, in_specs=placed, out_specs=P("win", None, None, None), check_vma=False,
    )
```

time: 108 us -> 43.6 us (0.40)
  the two profiles are of different devices: /device:TPU:0 before, /device:TPU:17 now
where the time goes in v1:
time: 43.6 us; the launch traced here: 43.4 us
  Pallas kernels  41.1 us (94%)
  local copies, waits for them, and re-layouts  2.31 us (5%)
    pallas_call x1, Pallas kernels, local(): pl.pallas_call(functools.partial(kernel, n, size, min(POINTS, count)), ou...  41.1 us
    unnamed x1, local copies, waits for them, and re-layouts  2.31 us

profile of v1, /device:TPU:17, one launch (start us, length us, event | category | flops | bytes accessed | tf_op | source)
XLA Modules:
  0.0 43.4 jit_solution(1579873277747192268)
XLA Ops:
  0.0 41.1 %shard_map.55 = f32[2,128,1024]{2,1,0:T(8,128)} custom-call(s32[2,32768]{1,0:T(2,128)} %rows_hbm.1, s32[2,32768]{1,0:T(2,128)} %cols_hbm.1, s32[2,32768]{1,0:T(2,128)} %chans_hbm.1, bf16[2,32768]{1,0:T(2,128)(2,1)} %weights_hbm.1, f32[2,4]{1,0:T(2,128)} %decay_ref.1), custom_call_target="tpu_custom_call" | custom-call | tf_op jit(solution)/shard_map/pallas_call | solution.py:245
  41.1 2.3 %copy.7 = f32[2,4,32,1024]{3,2,1,0:T(8,128)} copy(f32[2,4,32,1024]{3,2,1,0:T(8,128)} %bitcast.1) | data formatting | bytes 2097152

commit v2 on v1

--- a/solution.py
+++ b/solution.py
@@ -15,7 +15,7 @@
 SUBLANES = 8
 PART = 256
 CHUNK = 512
-POINTS = 8192
+POINTS = 16384
 MESH = pl.DeviceIdType.MESH
 
 
@@ -60,11 +60,9 @@
     group, member = lax.div(me, size), lax.rem(me, size)
     mate = lambda k: group * size + lax.rem(member + k, size)
 
+    sources = ((cols_hbm, cols_ref), (chans_hbm, chans_ref), (rows_hbm, rows_ref), (weights_hbm, weights_ref))
     loads = [
-        pltpu.make_async_copy(source, target, load_sem.at[i])
-        for i, (source, target) in enumerate(
-            ((cols_hbm, cols_ref), (chans_hbm, chans_ref), (rows_hbm, rows_ref), (weights_hbm, weights_ref))
-        )
+        pltpu.make_async_copy(source, target, load_sem.at[i]) for i, (source, target) in enumerate(sources)
     ]
     for load in loads:
         load.start()
@@ -78,12 +76,14 @@
     hist[...] = jnp.zeros(hist.shape, jnp.float32)
     for load in loads:
         load.wait()
-    pl.semaphore_wait(barrier, size - 1 + groups - 1)
+
+    def sent(ref, chunk):
+        return ref if chunk == 0 else ref.at[:, pl.ds(0, CHUNK)]
 
     def go(chunk, k):
         peer = lax.rem(member + k, size)
         return pltpu.make_async_remote_copy(
-            src_ref=stage.at[chunk, peer], dst_ref=inbox.at[chunk, member],
+            src_ref=sent(stage.at[chunk, peer], chunk), dst_ref=sent(inbox.at[chunk, member], chunk),
             send_sem=go_send.at[chunk, k], recv_sem=go_recv.at[chunk, member],
             device_id=(mate(k),), device_id_type=MESH,
         )
@@ -91,14 +91,14 @@
     def come(chunk, k):
         peer = lax.rem(member + k, size)
         return pltpu.make_async_remote_copy(
-            src_ref=stage.at[chunk, peer], dst_ref=inbox.at[chunk, peer],
+            src_ref=sent(stage.at[chunk, peer], chunk), dst_ref=sent(inbox.at[chunk, peer], chunk),
             send_sem=go_send.at[chunk, k], recv_sem=go_recv.at[chunk, peer],
             device_id=(mate(k),), device_id_type=MESH,
         )
 
     def up(chunk, k, slot):
         return pltpu.make_async_remote_copy(
-            src_ref=total.at[chunk], dst_ref=earlier.at[chunk, slot],
+            src_ref=sent(total.at[chunk], chunk), dst_ref=sent(earlier.at[chunk, slot], chunk),
             send_sem=up_send.at[chunk, k], recv_sem=up_recv.at[chunk, slot],
             device_id=(lax.rem(me + k * size, n),), device_id_type=MESH,
         )
@@ -129,10 +129,14 @@
                 running = decay_ref[window, channel] * running + hist[window, chunk, at, :]
                 factor = factor * decay_ref[window, channel]
             stage[chunk, p, :, :CHUNK] = running
-            stage[chunk, p, :, CHUNK:] = factor
+            if chunk == 0:
+                stage[chunk, p, :, CHUNK:] = factor
+        if chunk == 0:
+            pl.semaphore_wait(barrier, size - 1 + groups - 1)
         for k in range(1, size):
             go(chunk, k).start()
-        inbox[chunk, member] = stage[chunk, member]
+        wide = CHUNK if chunk else CHUNK + LANES
+        inbox[chunk, member, :, :wide] = stage[chunk, member, :, :wide]
 
     def scan_group(chunk):
         for k in range(1, size):
@@ -141,12 +145,15 @@
         factor = jnp.ones((piece, LANES), jnp.float32)
         for m in range(size):
             back[chunk, m] = running
-            spread[chunk, m] = factor
-            by = inbox[chunk, m, :, CHUNK:]
+            by = inbox[0, m, :, CHUNK:]
+            if chunk == 0:
+                spread[m] = factor
             running = across(by, CHUNK) * running + inbox[chunk, m, :, :CHUNK]
-            factor = factor * by
+            if chunk == 0:
+                factor = factor * by
         total[chunk, :, :CHUNK] = running
-        total[chunk, :, CHUNK:] = factor
+        if chunk == 0:
+            total[chunk, :, CHUNK:] = factor
         for k in range(1, groups):
 
             @pl.when(group + k < groups)
@@ -161,14 +168,14 @@
                 @pl.when(g < group)
                 def _():
                     up(chunk, 1, g).wait_recv()
-                    by = earlier[chunk, g, :, CHUNK:]
+                    by = earlier[0, g, :, CHUNK:]
                     carried[...] = across(by, CHUNK) * carried[...] + earlier[chunk, g, :, :CHUNK]
 
             @pl.when(group > 0)
             def _():
                 before = carried[...]
                 for m in range(size):
-                    back[chunk, m] += across(spread[chunk, m], CHUNK) * before
+                    back[chunk, m] += across(spread[m], CHUNK) * before
 
         for k in range(1, size):
             give(chunk, k).start()
@@ -198,12 +205,11 @@
     for chunk in range(chunks):
         for window in range(windows):
 
+            if chunk > 0 and window == windows - 1:
+                scan_group(chunk - 1)
+
             def step(i, carry):
-                if chunk > 0 and window == windows - 1:
-
-                    @pl.when(i == steps // 4)
-                    def _():
-                        scan_group(chunk - 1)
+                if chunk > 0 and window == windows - 1 and steps > 1:
 
                     @pl.when(i == steps - 1)
                     def _():
@@ -217,6 +223,8 @@
             lax.fori_loop(0, steps, step, 0)
         send_sums(chunk)
         if chunk > 0:
+            if steps == 1:
+                send_back(chunk - 1)
             finish(chunk - 1)
     scan_group(chunks - 1)
     send_back(chunks - 1)
@@ -258,7 +266,7 @@
             pltpu.VMEM((chunks, piece, wide), jnp.float32),
             pltpu.VMEM((chunks, groups, piece, wide), jnp.float32),
             pltpu.VMEM((piece, CHUNK), jnp.float32),
-            pltpu.VMEM((chunks, size, piece, LANES), jnp.float32),
+            pltpu.VMEM((size, piece, LANES), jnp.float32),
             pltpu.VMEM((chunks, size, piece, CHUNK), jnp.float32),
             pltpu.VMEM((chunks, size, piece, CHUNK), jnp.float32),
             dma((4,)),

time: 43.6 us -> 39.2 us (0.90)
  Pallas kernels: 41.1 us -> 36.7 us
    pallas_call x1, Pallas kernels: 41.1 us -> 36.7 us  [local(): pl.pallas_call(functools.partial(kernel, n, size, min(POINTS, count)), ou...]
where the time goes in v2:
time: 39.2 us; the launch traced here: 39 us
  Pallas kernels  36.7 us (94%)
  local copies, waits for them, and re-layouts  2.31 us (6%)
    pallas_call x1, Pallas kernels, local(): pl.pallas_call(functools.partial(kernel, n, size, min(POINTS, count)), ou...  36.7 us
    unnamed x1, local copies, waits for them, and re-layouts  2.31 us

profile of v2, /device:TPU:17, one launch (start us, length us, event | category | flops | bytes accessed | tf_op | source)
XLA Modules:
  0.0 39.0 jit_solution(14408482630291035745)
XLA Ops:
  0.0 36.7 %shard_map.55 = f32[2,128,1024]{2,1,0:T(8,128)} custom-call(s32[2,32768]{1,0:T(2,128)} %rows_hbm.1, s32[2,32768]{1,0:T(2,128)} %cols_hbm.1, s32[2,32768]{1,0:T(2,128)} %chans_hbm.1, bf16[2,32768]{1,0:T(2,128)(2,1)} %weights_hbm.1, f32[2,4]{1,0:T(2,128)} %decay_ref.1), custom_call_target="tpu_custom_call" | custom-call | tf_op jit(solution)/shard_map/pallas_call | solution.py:253
  36.7 2.3 %copy.7 = f32[2,4,32,1024]{3,2,1,0:T(8,128)} copy(f32[2,4,32,1024]{3,2,1,0:T(8,128)} %bitcast.1) | data formatting | bytes 2097152
